TPU v7x, 32 devices: a whole 2x2x4 slice. The times are simulated.
32 devices in a mesh: batch: 8 (over y, x, core), rows: 4 (over z).
Axes of the slice: x: 2, y: 2, z: 4, core: 2. Of those that a mesh axis runs over, the one named last changes fastest.
Arguments:
- fine_level: bfloat16 [8, 32, 192, 384], P('batch', 'rows'), may hold values from -40 to 40
- middle_level: bfloat16 [8, 16, 96, 384], P('batch', 'rows'), may hold values from -40 to 40
- coarse_level: bfloat16 [8, 8, 48, 384], P('batch', 'rows'), may hold values from -40 to 40
- two_input_weights: float32 [2, 3, 2], replicated, may hold values from 0.5 to 2
- three_input_weights: float32 [2, 3], replicated, may hold values from 0.5 to 2
- depthwise: bfloat16 [2, 4, 3, 3, 384], replicated, may hold values from -2 to 2
- pointwise: bfloat16 [2, 4, 384, 384], replicated, may hold values from -0.3125 to 0.3125
- bn_gain: float32 [2, 4, 384], replicated, may hold values from 0.5 to 1.5
- bn_bias: float32 [2, 4, 384], replicated, may hold values from -3 to 3
Outputs:
- fine_result: bfloat16 [8, 32, 192, 384], P('batch', 'rows')
- middle_result: bfloat16 [8, 16, 96, 384], P('batch', 'rows')
- coarse_result: bfloat16 [8, 8, 48, 384], P('batch', 'rows')
All inputs are finite; a program needn't handle non-finite values.
Results may differ from a plain program's by a relative error of at most 0.025.
Values may be sent and summed in bfloat16 or wider, within the bound.
A program may use at most 64 MiB of HBM per device.

v0:
```python
import functools

import jax
import jax.numpy as jnp
from jax import lax
from jax.experimental import pallas as pl
from jax.experimental.pallas import tpu as pltpu
from jax.sharding import PartitionSpec as P

LAYERS = 2
NODES = 4
MESH = pl.DeviceIdType.MESH
F32 = jnp.float32
BF16 = jnp.bfloat16
PAD = 8
LANES = 256


def permutation(size, phases, inverse):
    part = size // phases
    natural = lax.broadcasted_iota(jnp.int32, (size, size), 0 if inverse else 1)
    ordered = lax.broadcasted_iota(jnp.int32, (size, size), 1 if inverse else 0)
    phase = jnp.zeros((size, size), jnp.int32)
    for p in range(1, phases):
        phase = phase + jnp.where(ordered >= p * part, 1, 0)
    hit = natural == phases * (ordered - phase * part) + phase
    return jnp.where(hit, 1.0, 0.0).astype(BF16)


def kernel(
    nb, nr,
    fine, mid, top, w2_in, w3_in, dw_in, pw_in, gain_in, bias_in,
    out_f, out_m, out_t,
    afine, amid, w2, w3, pw, dw, gain, bias, tapx, act, sp, tmp, raw_f, raw_d, raw_m, raw_t,
    cpf, cpm, pool_f, pool_m, nf, nf_s, nf_r, nm, nm_s, nm_r, nt,
    edge_d, red_d, edge_m, red_m, up_f, dn_f, up_m, dn_m, rup_f, rdn_f, rup_m, rdn_m, rup_t, rdn_t, edge_t,
    perm_f, perm_m, stat_b,
    sb_s, sb_r, h_s, h_r, loc, wave,
):
    b_me = lax.axis_index("batch")
    r_me = lax.axis_index("rows")

    has_up = r_me > 0
    has_dn = r_me < nr - 1
    above = jnp.maximum(r_me - 1, 0)
    below = jnp.minimum(r_me + 1, nr - 1)

    def signal(sem, where):
        pl.semaphore_signal(sem, inc=1, device_id=where, device_id_type=MESH)

    barrier = pltpu.get_barrier_semaphore()
    for guard, row in ((has_up, above), (has_dn, below)):
        @pl.when(guard)
        def _():
            signal(barrier, {"rows": row})

    for d in range(1, nb):
        signal(barrier, {"batch": lax.rem(b_me + d, nb)})

    def near_ready():
        peers = jnp.minimum(r_me, 1) + jnp.minimum(nr - 1 - r_me, 1)
        pl.semaphore_wait(barrier, nb - 1 + peers)

    waves = ((has_up, has_dn, below), (has_dn, has_up, above))

    def wave_open():
        for k, (came, goes, row) in enumerate(waves):
            @pl.when(goes & jnp.logical_not(came))
            def _():
                signal(wave.at[k], {"rows": row})

    def wave_pass():
        for k, (came, goes, row) in enumerate(waves):
            @pl.when(goes & came)
            def _():
                pl.semaphore_wait(wave.at[k], 1)
                signal(wave.at[k], {"rows": row})

    def wave_close():
        for k, (came, goes, row) in enumerate(waves):
            @pl.when(came & jnp.logical_not(goes))
            def _():
                pl.semaphore_wait(wave.at[k], 1)

    Rf, Wf, C = fine.shape[1:]
    Rm, Wm = mid.shape[1:3]
    Rt, J = top.shape[1:3]
    Pf, Pm = Wf // J, Wm // J
    H = J // 2

    loads = [
        pltpu.make_async_copy(mid.at[0], amid, loc.at[0]),
        pltpu.make_async_copy(top.at[0], nt.at[0, pl.ds(1, Rt)], loc.at[1]),
        pltpu.make_async_copy(dw_in, dw, loc.at[2]),
        pltpu.make_async_copy(gain_in, gain, loc.at[3]),
        pltpu.make_async_copy(bias_in, bias, loc.at[4]),
        pltpu.make_async_copy(fine.at[0], afine, loc.at[5]),
        pltpu.make_async_copy(pw_in, pw, loc.at[6]),
        pltpu.make_async_copy(w2_in, w2, loc.at[7]),
        pltpu.make_async_copy(w3_in, w3, loc.at[8]),
    ]
    for copy in loads[7:] + loads[:7]:
        copy.start()

    def message(k, src, dst, up):
        return pltpu.make_async_remote_copy(
            src_ref=src, dst_ref=dst, send_sem=h_s.at[k], recv_sem=h_r.at[k],
            device_id={"rows": above if up else below}, device_id_type=MESH,
        )

    def send(k, src, dst, up):
        @pl.when(has_up if up else has_dn)
        def _():
            message(k, src, dst, up).start()

    def arrive(k, src, dst, up):
        @pl.when(has_dn if up else has_up)
        def _():
            message(k, src, dst, up).wait_recv()

        @pl.when(has_up if up else has_dn)
        def _():
            message(k, src, dst, up).wait_send()

    def share(node, db, dr, rows):
        me = b_me * nr + r_me
        return pltpu.make_async_remote_copy(
            src_ref=stat_b.at[node, me], dst_ref=stat_b.at[node, me],
            send_sem=sb_s.at[node % 2, db * nr + dr], recv_sem=sb_r.at[node, db * nr + dr],
            device_id={"batch": lax.rem(b_me + db, nb), "rows": rows},
            device_id_type=MESH,
        )

    def stats_begin(node, total, square, count):
        me = b_me * nr + r_me
        mean = total / count
        sent = mean.astype(BF16).astype(F32)
        stat_b[node, me] = jnp.concatenate(
            [sent, square / count - sent * (2.0 * mean - sent)], axis=0
        ).astype(BF16)
        side = r_me // ((nr + 1) // 2)
        for k in range(nr):
            rows = (1 - side) * (nr - 1 - k) + side * k
            dr = lax.rem(rows - r_me + nr, nr)
            for db in range(nb - 1, 0, -1):
                share(node, db, dr, rows).start()
            if k == 0:
                for dr in range(nr - 1, 0, -1):
                    share(node, 0, dr, lax.rem(r_me + dr, nr)).start()

        if node:
            settle(node - 1)

    def shares(node):
        return [
            share(node, d // nr, d % nr, lax.rem(r_me + d % nr, nr)) for d in range(1, nb * nr)
        ]

    def settle(node):
        for copy in shares(node):
            copy.wait_send()

    def stats_end(node, layer, which):
        for copy in shares(node):
            copy.wait_recv()
        parts = stat_b[node].astype(F32)
        both = jnp.sum(parts, axis=0) / (nb * nr)
        center = both[0:1]
        squares = jnp.sum(parts * parts, axis=0)[0:1] / (nb * nr)
        spread = both[1:2] + (squares - center * center)
        scale = lax.rsqrt(spread + 1e-05) * gain[layer, which : which + 1, :]
        return scale, bias[layer, which : which + 1, :] - center * scale

    def normal(x, stats):
        return x * stats[0] + stats[1]

    def scaled(stats, weight):
        return stats[0] * weight, stats[1] * weight

    def coefficients(weights):
        total = weights[0]
        for w in weights[1:]:
            total = total + w
        inverse = 0.5 / (total + 0.0001)
        return [jnp.broadcast_to(w * inverse, (1, C)) for w in weights]

    place = lax.broadcasted_iota(jnp.int32, (J, C), 0)

    def put(row, plane, a):
        act[row, plane, :, pl.ds(0, C)] = a[0:H].astype(BF16)
        act[row, plane, :, pl.ds(C, C)] = a[H:J].astype(BF16)

    def activate(row, p, phases, half, valid=None):
        a = half + half * jnp.tanh(half)
        if valid is not None:
            a = jnp.where(valid, a, 0.0)
        put(row, p + 1, a)
        if p == phases - 1:
            put(row, 0, jnp.where(place == 0, 0.0, pltpu.roll(a, 1, 0)))
        if p == 0:
            put(row, phases + 1, jnp.where(place == J - 1, 0.0, pltpu.roll(a, J - 1, 0)))

    def depthwise(node, r, phases):
        for c in range(2 * C // LANES):
            lanes = pl.ds(c * LANES, LANES)
            taps = [[tapx[node, 3 * i + j, :, lanes] for j in range(3)] for i in range(3)]
            for s in range(H // 8):
                near = [
                    [act[r + i, q, pl.ds(8 * s, 8), lanes] for q in range(phases + 2)]
                    for i in range(3)
                ]
                for p in range(phases):
                    total = None
                    for i in range(3):
                        for j in range(3):
                            term = near[i][p + j] * taps[i][j]
                            total = term if total is None else total + term
                    at = (r * phases + p) * H + 8 * s
                    sp[pl.ds(at, 8), lanes] = total

    def pointwise(layer, which, first, rows, phases, dst, shift=0):
        total = jnp.zeros((1, C), F32)
        square = jnp.zeros((1, C), F32)
        span = pl.ds(first * phases * H, rows * phases * H)
        for h in range(2):
            y = jnp.dot(
                sp[span, pl.ds(h * C, C)], pw[layer, which], preferred_element_type=F32
            )
            for r in range(rows):
                for p in range(phases):
                    a = (r * phases + p) * H
                    dst[first + r + shift, p, pl.ds(h * H, H), :] = y[a : a + H]
            total = total + jnp.sum(y, axis=0, keepdims=True)
            square = square + jnp.sum(y * y, axis=0, keepdims=True)
        return total, square

    def convolve(layer, which, first, rows, phases, dst, shift=0):
        for r in range(first, first + rows):
            depthwise(NODES * layer + which, r, phases)
        return pointwise(layer, which, first, rows, phases, dst, shift)

    def loop(lo, hi, body):
        lax.fori_loop(lo, hi, lambda i, c: (body(i), c)[1], 0)

    def column_pool(src, row, q, phases):
        a = jnp.maximum(src[row, 2 * q, pl.ds(0, J), :], src[row, 2 * q + 1, pl.ds(0, J), :])
        if 2 * q + 2 < phases:
            return jnp.maximum(a, src[row, 2 * q + 2, pl.ds(0, J), :])
        return jnp.maximum(a, src[row, 0, pl.ds(1, J), :])

    perm_m[0] = permutation(Wm, Pm, False)
    loads[7].wait()
    loads[8].wait()
    mix = []
    for layer in range(LAYERS):
        pairs = [
            coefficients([w2[layer, i : i + 1, k : k + 1] for i in range(2)]) for k in range(3)
        ]
        mix.append(pairs + [coefficients([w3[layer : layer + 1, i : i + 1] for i in range(3)])])
    loads[0].wait()

    def order_mid(e, side=None):
        y = jnp.dot(perm_m[0], amid[e], preferred_element_type=F32)
        for p in range(Pm):
            part = y[p * J : (p + 1) * J]
            nm[e + 1, p] = part * mix[0][0][0]
            if side is not None:
                nm_s[side, p] = part.astype(BF16)

    order_mid(0, 0)
    order_mid(Rm - 1, 1)
    loads[1].wait()
    near_ready()
    wave_open()
    first = [
        (0, nt.at[0, 1], nt.at[0, Rt + 1], True),
        (1, nt.at[0, Rt], nt.at[0, 0], False),
        (2, nm_s.at[0], nm_r.at[1], True),
        (3, nm_s.at[1], nm_r.at[0], False),
    ]
    for m in first:
        send(*m)
    loop(1, Rm - 1, order_mid)
    perm_f[0] = permutation(Wf, Pf, False)
    loads[2].wait()
    for layer in range(LAYERS):
        for i in range(3):
            for j in range(3):
                taps = dw[layer, i, j].astype(F32)
                for n in range(NODES):
                    tap = jnp.broadcast_to(taps[n : n + 1], (8, C)).astype(BF16)
                    tapx[NODES * layer + n, 3 * i + j, :, pl.ds(0, C)] = tap
                    tapx[NODES * layer + n, 3 * i + j, :, pl.ds(C, C)] = tap
    loads[5].wait()

    def order_fine(e, side=None):
        y = jnp.dot(perm_f[0], afine[e], preferred_element_type=F32)
        for p in range(Pf):
            part = y[p * J : (p + 1) * J]
            nf[e + 1, p] = part * mix[0][1][0]
            if side is not None:
                nf_s[0, side, p] = part.astype(BF16)

    order_fine(0, 0)
    order_fine(Rf - 1, 1)
    fine_rows = []
    for k in range(LAYERS):
        for p in range(0, Pf, Pf // 2):
            at = 4 + 4 * k + 2 * (p > 0)
            half = pl.ds(p, Pf // 2)
            fine_rows.append([
                (at, nf_s.at[k, 0, half], nf_r.at[k, 1, half], True),
                (at + 1, nf_s.at[k, 1, half], nf_r.at[k, 0, half], False),
            ])
    for m in fine_rows[0] + fine_rows[1]:
        send(*m)
    loop(1, Rf - 1, order_fine)
    wave_pass()
    perm_f[1] = permutation(Wf, Pf, True)
    perm_m[1] = permutation(Wm, Pm, True)
    raw_f[:, :, J : J + PAD, :] = jnp.full((Rf, Pf, PAD, C), -jnp.inf, F32)
    raw_m[:, :, J : J + PAD, :] = jnp.full((Rm, Pm, PAD, C), -jnp.inf, F32)
    for copy in (loads[3], loads[4], loads[6]):
        copy.wait()

    for layer in range(LAYERS):
        last = layer == LAYERS - 1
        base = NODES * layer
        hb = 4 + 4 * LAYERS + 11 * layer

        c0, c1, c3, c2 = mix[layer]

        def act0(e, valid=None):
            coarse = nt[layer, (e + 1) // 2].astype(F32) * c0[1]
            for p in range(Pm):
                activate(e, p, Pm, nm[e, p] + coarse, valid)

        loop(1, Rm + 1, act0)
        if layer == 0:
            for r in range(1, Rm - 1):
                depthwise(base, r, Pm)
            for m in first:
                arrive(*m)
            for p in range(Pm):
                nm[0, p] = nm_r[0, p].astype(F32) * c0[0]
                nm[Rm + 1, p] = nm_r[1, p].astype(F32) * c0[0]
        act0(0, has_up)
        act0(Rm + 1, has_dn)
        if layer == 0:
            wave_close()
            for r in (0, Rm - 1):
                depthwise(base, r, Pm)
            t, s = pointwise(layer, 0, 0, Rm, Pm, raw_d, 1)
        else:
            t, s = convolve(layer, 0, 0, Rm, Pm, raw_d, 1)
        stats_begin(base, t, s, float(Rm * Wm))
        edge_d[0] = raw_d[1].astype(BF16)
        edge_d[1] = raw_d[Rm].astype(BF16)
        edge = [
            (hb, edge_d.at[0], red_d.at[layer, 1], True),
            (hb + 1, edge_d.at[1], red_d.at[layer, 0], False),
        ]
        for m in edge:
            send(*m)
        for m in edge:
            arrive(*m)
        raw_d[0] = red_d[layer, 0].astype(F32)
        raw_d[Rm + 1] = red_d[layer, 1].astype(F32)
        for m in fine_rows[2 * layer] + fine_rows[2 * layer + 1]:
            arrive(*m)
        for p in range(Pf):
            nf[0, p] = nf_r[layer, 0, p].astype(F32) * c1[0]
            nf[Rf + 1, p] = nf_r[layer, 1, p].astype(F32) * c1[0]
        sd = scaled(stats_end(base, layer, 0), c1[1])

        def norm_d(e):
            for p in range(Pm):
                raw_d[e, p] = normal(raw_d[e, p], sd)

        loop(0, Rm + 2, norm_d)

        def act1(e, valid=None):
            for p in range(Pf):
                activate(e, p, Pf, nf[e, p] + raw_d[(e + 1) // 2, p // 2], valid)

        def pool_cols_f(r):
            for q in range(Pm):
                cpf[r, q] = column_pool(raw_f, r, q, Pf)

        part = Rf // 2
        edge = [
            (hb + 2, up_f.at[0], rup_f.at[layer, 0], True),
            (hb + 3, up_f.at[1], rup_f.at[layer, 1], True),
            (hb + 4, dn_f, rdn_f.at[layer], False),
        ]
        act1(0, has_up)
        loop(1, part + 2, act1)
        t, s = convolve(layer, 1, 0, part, Pf, raw_f)
        pool_cols_f(0)
        up_f[0] = cpf[0].astype(BF16)
        send(*edge[0])
        loop(part + 2, Rf + 1, act1)
        act1(Rf + 1, has_dn)
        t2, s2 = convolve(layer, 1, part, Rf - part, Pf, raw_f)
        stats_begin(base + 1, t + t2, s + s2, float(Rf * Wf))
        pool_cols_f(1)
        pool_cols_f(2)
        up_f[1] = jnp.maximum(jnp.maximum(cpf[0], cpf[1]), cpf[2]).astype(BF16)
        send(*edge[1])
        pool_cols_f(Rf - 2)
        pool_cols_f(Rf - 1)
        bottom = jnp.maximum(cpf[Rf - 2], cpf[Rf - 1])
        dn_f[...] = bottom.astype(BF16)
        pool_f[Rm] = bottom
        send(*edge[2])
        loop(3, Rf - 2, pool_cols_f)

        def pool_rows_f(i):
            pool_f[i + 1] = jnp.maximum(
                jnp.maximum(cpf[2 * i], cpf[2 * i + 1]), cpf[2 * i + 2]
            )

        loop(0, Rm - 1, pool_rows_f)
        ratio_m = c2[0] / c0[0]
        ratio_d = c2[1] / c1[1]

        def join_d(e):
            for p in range(Pm):
                raw_d[e, p] = nm[e, p] * ratio_m + raw_d[e, p] * ratio_d

        loop(0, Rm + 2, join_d)
        for m in edge:
            arrive(*m)
        pool_f[0] = jnp.maximum(rdn_f[layer].astype(F32), cpf[0])
        pool_f[Rm] = jnp.maximum(
            pool_f[Rm], jnp.where(has_dn, rup_f[layer, 0].astype(F32), -jnp.inf)
        )
        pool_f[Rm + 1] = rup_f[layer, 1].astype(F32)
        sf = stats_end(base + 1, layer, 1)
        sw = scaled(sf, c2[2])

        def act2(e, valid=None):
            for p in range(Pm):
                activate(e, p, Pm, raw_d[e, p] + normal(pool_f[e, p], sw), valid)

        act2(0, has_up)
        act2(Rm + 1, has_dn)
        loop(1, Rm + 1, act2)
        t, s = convolve(layer, 2, 0, Rm, Pm, raw_m)
        stats_begin(base + 2, t, s, float(Rm * Wm))

        def pool_cols_m(r):
            cpm[r] = column_pool(raw_m, r, 0, Pm)

        loop(0, Rm, pool_cols_m)
        up_m[0] = cpm[0].astype(BF16)
        up_m[1] = jnp.maximum(jnp.maximum(cpm[0], cpm[1]), cpm[2]).astype(BF16)
        bottom = jnp.maximum(cpm[Rm - 2], cpm[Rm - 1])
        dn_m[...] = bottom.astype(BF16)
        pool_m[Rt] = bottom
        edge = [
            (hb + 5, up_m, rup_m.at[layer], True),
            (hb + 6, dn_m, rdn_m.at[layer], False),
        ]
        for m in edge:
            send(*m)

        def pool_rows_m(i):
            pool_m[i + 1] = jnp.maximum(
                jnp.maximum(cpm[2 * i], cpm[2 * i + 1]), cpm[2 * i + 2]
            )

        loop(0, Rt - 1, pool_rows_m)
        rows = []
        if not last:
            for p in range(Pm):
                edge_m[0, p] = raw_m[0, p, pl.ds(0, J), :].astype(BF16)
                edge_m[1, p] = raw_m[Rm - 1, p, pl.ds(0, J), :].astype(BF16)
            rows = [
                (hb + 7, edge_m.at[0], red_m.at[layer, 1], True),
                (hb + 8, edge_m.at[1], red_m.at[layer, 0], False),
            ]
            for m in rows:
                send(*m)

        if last:

            def finish_f(r):
                for p in range(Pf):
                    tmp[pl.ds(p * J, J), :] = normal(raw_f[r, p, pl.ds(0, J), :], sf).astype(BF16)
                out_f[0, r] = jnp.dot(
                    perm_f[1], tmp[...], preferred_element_type=F32
                ).astype(BF16)

        else:

            sn = scaled(sf, mix[layer + 1][1][0])
            for p in range(Pf):
                for side, r in enumerate((0, Rf - 1)):
                    nf_s[layer + 1, side, p] = normal(
                        raw_f[r, p, pl.ds(0, J), :], sf
                    ).astype(BF16)

            def finish_f(r):
                for p in range(Pf):
                    nf[r + 1, p] = normal(raw_f[r, p, pl.ds(0, J), :], sn)

        loop(0, Rf, finish_f)
        if not last:
            for m in fine_rows[2 * layer + 2]:
                send(*m)
        for m in edge:
            arrive(*m)
        pool_m[0] = jnp.maximum(rdn_m[layer].astype(F32), cpm[0])
        pool_m[Rt] = jnp.maximum(
            pool_m[Rt], jnp.where(has_dn, rup_m[layer, 0].astype(F32), -jnp.inf)
        )
        pool_m[Rt + 1] = rup_m[layer, 1].astype(F32)
        sm = stats_end(base + 2, layer, 2)

        sw = scaled(sm, c3[1])

        for e in range(Rt + 2):
            half = nt[layer, e].astype(F32) * c3[0] + normal(pool_m[e], sw)
            valid = has_up if e == 0 else has_dn if e == Rt + 1 else None
            activate(e, 0, 1, half, valid)
        t, s = convolve(layer, 3, 0, Rt, 1, raw_t)
        stats_begin(base + 3, t, s, float(Rt * J))
        if last:

            def finish_m(r):
                for p in range(Pm):
                    tmp[pl.ds(p * J, J), :] = normal(raw_m[r, p, pl.ds(0, J), :], sm).astype(BF16)
                out_m[0, r] = jnp.dot(
                    perm_m[1], tmp[pl.ds(0, Wm), :], preferred_element_type=F32
                ).astype(BF16)

            loop(0, Rm, finish_m)
            st = stats_end(base + 3, layer, 3)
            for r in range(Rt):
                out_t[0, r] = normal(raw_t[r, 0], st).astype(BF16)
            settle(base + 3)
        else:
            edge_t[0] = raw_t[0, 0].astype(BF16)
            edge_t[1] = raw_t[Rt - 1, 0].astype(BF16)
            edge = [
                (hb + 9, edge_t.at[0], rup_t.at[layer], True),
                (hb + 10, edge_t.at[1], rdn_t.at[layer], False),
            ]
            for m in edge + fine_rows[2 * layer + 3]:
                send(*m)

            sn = scaled(sm, mix[layer + 1][0][0])

            def finish_m(r):
                for p in range(Pm):
                    nm[r + 1, p] = normal(raw_m[r, p, pl.ds(0, J), :], sn)

            loop(0, Rm, finish_m)
            for m in edge + rows:
                arrive(*m)
            for p in range(Pm):
                nm[0, p] = normal(red_m[layer, 0, p].astype(F32), sn)
                nm[Rm + 1, p] = normal(red_m[layer, 1, p].astype(F32), sn)
            st = stats_end(base + 3, layer, 3)
            nt[layer + 1, 0] = normal(rdn_t[layer].astype(F32), st).astype(BF16)
            for r in range(Rt):
                nt[layer + 1, r + 1] = normal(raw_t[r, 0], st).astype(BF16)
            nt[layer + 1, Rt + 1] = normal(rup_t[layer].astype(F32), st).astype(BF16)


def flush(a, b, c, out_a, out_b, out_c, sems):
    parts = [(b, out_b), (c, out_c)]
    rows = a.shape[1] // 4
    for k in range(4):
        at = pl.ds(k * rows, rows)
        parts.append((a.at[:, at], out_a.at[:, at]))
    copies = [
        pltpu.make_async_copy(src, dst, sems.at[k]) for k, (src, dst) in enumerate(parts)
    ]
    for copy in copies:
        copy.start()
    for copy in copies:
        copy.wait()


def body(nb, nr, fine, mid, top, w2, w3, dw, pw, gain, bias):
    _, Rf, Wf, C = fine.shape
    _, Rm, Wm, _ = mid.shape
    _, Rt, J, _ = top.shape
    Pf, Pm = Wf // J, Wm // J
    H = J // 2
    assert fine.shape[0] == 1 and Pf == 4 and Pm == 2 and J % 16 == 0
    assert Rf == 2 * Rm and Rm == 2 * Rt and Rt >= 2 and 2 * C % LANES == 0
    L = LAYERS
    V = pltpu.VMEM
    dw = jnp.transpose(dw, (0, 2, 3, 1, 4))
    w2 = jnp.swapaxes(w2, 1, 2)
    messages = 4 + 15 * L
    scratch = [
        V((Rf, Wf, C), BF16), V((Rm, Wm, C), BF16), V(w2.shape, F32), V(w3.shape, F32),
        V(pw.shape, BF16), V(dw.shape, BF16), V(gain.shape, F32), V(bias.shape, F32),
        V((L * NODES, 9, 8, 2 * C), BF16),
        V((Rf + 2, Pf + 2, H, 2 * C), BF16), V((Rf * Pf * H, 2 * C), BF16), V((Wf, C), BF16),
        V((Rf, Pf, J + PAD, C), F32), V((Rm + 2, Pm, J, C), F32),
        V((Rm, Pm, J + PAD, C), F32), V((Rt, 1, J, C), F32),
        V((Rf, Pm, J, C), F32), V((Rm, J, C), F32),
        V((Rm + 2, Pm, J, C), F32), V((Rt + 2, J, C), F32),
        V((Rf + 2, Pf, J, C), F32), V((L, 2, Pf, J, C), BF16), V((L, 2, Pf, J, C), BF16),
        V((Rm + 2, Pm, J, C), F32), V((2, Pm, J, C), BF16), V((2, Pm, J, C), BF16),
        V((L, Rt + 2, J, C), BF16),
        V((2, Pm, J, C), BF16), V((L, 2, Pm, J, C), BF16),
        V((2, Pm, J, C), BF16), V((L, 2, Pm, J, C), BF16),
        V((2, Pm, J, C), BF16), V((Pm, J, C), BF16), V((2, J, C), BF16), V((J, C), BF16),
        V((L, 2, Pm, J, C), BF16), V((L, Pm, J, C), BF16),
        V((L, 2, J, C), BF16), V((L, J, C), BF16),
        V((L, J, C), BF16), V((L, J, C), BF16), V((2, J, C), BF16),
        V((2, Wf, Wf), BF16), V((2, Wm, Wm), BF16),
        V((L * NODES, nb * nr, 2, C), BF16),
        pltpu.SemaphoreType.DMA((2, nb * nr)), pltpu.SemaphoreType.DMA((L * NODES, nb * nr)),
        pltpu.SemaphoreType.DMA((messages,)), pltpu.SemaphoreType.DMA((messages,)),
        pltpu.SemaphoreType.DMA((9,)), pltpu.SemaphoreType.REGULAR((2,)),
    ]
    hbm = pl.BlockSpec(memory_space=pl.ANY)
    vmem = pl.BlockSpec(memory_space=pltpu.VMEM)
    levels = pl.pallas_call(
        functools.partial(kernel, nb, nr),
        out_shape=[pltpu.VMEM(a.shape, BF16) for a in (fine, mid, top)],
        in_specs=[hbm] * 9,
        out_specs=[vmem, vmem, vmem],
        scratch_shapes=scratch,
        name="bifpn",
        compiler_params=pltpu.CompilerParams(
            collective_id=0, has_side_effects=True, vmem_limit_bytes=56 * 2**20
        ),
    )(fine, mid, top, w2, w3, dw, pw, gain, bias)
    return tuple(pl.pallas_call(
        flush,
        out_shape=[jax.ShapeDtypeStruct(a.shape, BF16) for a in levels],
        in_specs=[hbm, hbm, hbm],
        out_specs=[hbm, hbm, hbm],
        scratch_shapes=[pltpu.SemaphoreType.DMA((6,))],
        name="flush",
        compiler_params=pltpu.CompilerParams(vmem_limit_bytes=2**20),
    )(*levels))


def solution(mesh):
    level = P("batch", "rows", None, None)
    return jax.shard_map(
        functools.partial(body, mesh.shape["batch"], mesh.shape["rows"]),
        mesh=mesh,
        in_specs=(level,) * 3 + (P(),) * 6,
        out_specs=(level,) * 3,
        check_vma=False,
    )
```

profile of v0, /device:TPU:0, one launch (start us, length us, event | category | flops | bytes accessed | tf_op | source)
XLA Modules:
  0.0 62.3 jit_solution(2130332834544513836)
XLA Ops:
  0.6 60.5 %bifpn.1 = (bf16[1,8,192,384]{3,2,1,0:T(8,128)(2,1)S(1)}, bf16[1,4,96,384]{3,2,1,0:T(8,128)(2,1)S(1)}, bf16[1,2,48,384]{3,2,1,0:T(8,128)(2,1)S(1)}) custom-call(bf16[1,8,192,384]{3,2,1,0:T(8,128)(2,1)} %fine.1, bf16[1,4,96,384]{3,2,1,0:T(8,128)(2,1)} %mid.1, bf16[1,2,48,384]{3,2,1,0:T(8,128)(2,1)} %top.1, f32[2,2,3]{2,1,0:T(2,128)} %bitcast.3, ...), custom_call_target="tpu_custom_call" | custom-call | tf_op jit(solution)/shard_map/bifpn/pallas_call | solution.py:626
  61.1 1.2 %flush.1 = (bf16[1,8,192,384]{3,2,1,0:T(8,128)(2,1)}, bf16[1,4,96,384]{3,2,1,0:T(8,128)(2,1)}, bf16[1,2,48,384]{3,2,1,0:T(8,128)(2,1)}) custom-call(bf16[1,8,192,384]{3,2,1,0:T(8,128)(2,1)S(1)} %get-tuple-element.6.a, bf16[1,4,96,384]{3,2,1,0:T(8,128)(2,1)S(1)} %get-tuple-element.7.b, bf16[1,2,48,384]{3,2,1,0:T(8,128)(2,1)S(1)} %get-tuple-element.8.c), custom_call_target="tpu_custom_call" | custom-call | tf_op jit(solution)/shard_map/flush/pallas_call | solution.py:637
where the time goes:
time: 62.4 us; the launch traced here: 62.3 us
  Pallas kernels  61.6 us (99%)
  between operations  0.64 us (1%)
    pallas_call x1, Pallas kernels, body(): pl.pallas_call(functools.partial(kernel, nb, nr), out_shape=[pltpu.VMEM(a...  60.5 us

commit v1 on v0

--- a/solution.py
+++ b/solution.py
@@ -122,11 +122,10 @@
         def _():
             message(k, src, dst, up).wait_send()
 
-    def share(node, db, dr, rows):
-        me = b_me * nr + r_me
+    def share(node, db, rows, span):
         return pltpu.make_async_remote_copy(
-            src_ref=stat_b.at[node, me], dst_ref=stat_b.at[node, me],
-            send_sem=sb_s.at[node % 2, db * nr + dr], recv_sem=sb_r.at[node, db * nr + dr],
+            src_ref=stat_b.at[node, span, rows_sent], dst_ref=stat_b.at[node, span, rows_sent],
+            send_sem=sb_s.at[node % 2], recv_sem=sb_r.at[node],
             device_id={"batch": lax.rem(b_me + db, nb), "rows": rows},
             device_id_type=MESH,
         )
@@ -135,39 +134,40 @@
         me = b_me * nr + r_me
         mean = total / count
         sent = mean.astype(BF16).astype(F32)
-        stat_b[node, me] = jnp.concatenate(
-            [sent, square / count - sent * (2.0 * mean - sent)], axis=0
-        ).astype(BF16)
+        spread = square / count - sent * (2.0 * mean - sent)
+        tiles = [v[:, k : k + 128] for v in (sent, spread) for k in range(0, C, 128)]
+        tiles.append(jnp.zeros((stat_b.shape[2] - len(tiles), 128), F32))
+        stat_b[node, me] = jnp.concatenate(tiles, axis=0).astype(BF16)
         side = r_me // ((nr + 1) // 2)
+        mine = pl.ds(me, 1)
         for k in range(nr):
             rows = (1 - side) * (nr - 1 - k) + side * k
-            dr = lax.rem(rows - r_me + nr, nr)
             for db in range(nb - 1, 0, -1):
-                share(node, db, dr, rows).start()
+                share(node, db, rows, mine).start()
             if k == 0:
                 for dr in range(nr - 1, 0, -1):
-                    share(node, 0, dr, lax.rem(r_me + dr, nr)).start()
-
+                    share(node, 0, lax.rem(r_me + dr, nr), mine).start()
         if node:
             settle(node - 1)
 
-    def shares(node):
-        return [
-            share(node, d // nr, d % nr, lax.rem(r_me + d % nr, nr)) for d in range(1, nb * nr)
-        ]
+    others = pl.ds(0, nb * nr - 1)
+    rows_sent = pl.ds(0, 2 * C // 128)
 
     def settle(node):
-        for copy in shares(node):
-            copy.wait_send()
+        share(node, 1, r_me, others).wait_send()
 
     def stats_end(node, layer, which):
-        for copy in shares(node):
-            copy.wait_recv()
+        share(node, 1, r_me, others).wait_recv()
         parts = stat_b[node].astype(F32)
         both = jnp.sum(parts, axis=0) / (nb * nr)
-        center = both[0:1]
-        squares = jnp.sum(parts * parts, axis=0)[0:1] / (nb * nr)
-        spread = both[1:2] + (squares - center * center)
+        squares = jnp.sum(parts * parts, axis=0) / (nb * nr)
+        deep = C // 128
+
+        def lane(x, k):
+            return jnp.concatenate([x[i : i + 1] for i in range(k, k + deep)], axis=1)
+
+        center = lane(both, 0)
+        spread = lane(both, deep) + (lane(squares, 0) - center * center)
         scale = lax.rsqrt(spread + 1e-05) * gain[layer, which : which + 1, :]
         return scale, bias[layer, which : which + 1, :] - center * scale
 
@@ -267,19 +267,38 @@
             if side is not None:
                 nm_s[side, p] = part.astype(BF16)
 
+    def act0(layer, e, valid=None):
+        coarse = nt[layer, (e + 1) // 2].astype(F32) * mix[layer][0][1]
+        for p in range(Pm):
+            activate(e, p, Pm, nm[e, p] + coarse, valid)
+
     order_mid(0, 0)
     order_mid(Rm - 1, 1)
     loads[1].wait()
+    act0(0, 1)
+    act0(0, Rm)
     near_ready()
     wave_open()
+    body = pl.ds(1, Pm)
     first = [
-        (0, nt.at[0, 1], nt.at[0, Rt + 1], True),
-        (1, nt.at[0, Rt], nt.at[0, 0], False),
-        (2, nm_s.at[0], nm_r.at[1], True),
-        (3, nm_s.at[1], nm_r.at[0], False),
+        (0, act.at[1, body], act.at[Rm + 1, body], True),
+        (1, act.at[Rm, body], act.at[0, body], False),
+    ]
+    top_rows = [
+        (2, nt.at[0, 1], nt.at[0, Rt + 1], True),
+        (3, nt.at[0, Rt], nt.at[0, 0], False),
+    ]
+    mid_rows = [
+        (4 + 15 * LAYERS, nm_s.at[0], nm_r.at[1], True),
+        (5 + 15 * LAYERS, nm_s.at[1], nm_r.at[0], False),
     ]
     for m in first:
         send(*m)
+    for guard, e in ((has_up, 0), (has_dn, Rm + 1)):
+        @pl.when(jnp.logical_not(guard))
+        def _():
+            act[e, body] = jnp.zeros((Pm, H, 2 * C), BF16)
+
     loop(1, Rm - 1, order_mid)
     perm_f[0] = permutation(Wf, Pf, False)
     loads[2].wait()
@@ -330,28 +349,27 @@
 
         c0, c1, c3, c2 = mix[layer]
 
-        def act0(e, valid=None):
-            coarse = nt[layer, (e + 1) // 2].astype(F32) * c0[1]
-            for p in range(Pm):
-                activate(e, p, Pm, nm[e, p] + coarse, valid)
-
-        loop(1, Rm + 1, act0)
         if layer == 0:
+            for e in range(2, Rm):
+                act0(0, e)
             for r in range(1, Rm - 1):
                 depthwise(base, r, Pm)
+            wave_close()
             for m in first:
                 arrive(*m)
-            for p in range(Pm):
-                nm[0, p] = nm_r[0, p].astype(F32) * c0[0]
-                nm[Rm + 1, p] = nm_r[1, p].astype(F32) * c0[0]
-        act0(0, has_up)
-        act0(Rm + 1, has_dn)
-        if layer == 0:
-            wave_close()
+            for e in (0, Rm + 1):
+                for plane, turn, gap in ((0, 1, 0), (Pm + 1, J - 1, J - 1)):
+                    near = act[e, Pm if plane == 0 else 1].astype(F32)
+                    row = jnp.concatenate([near[:, 0:C], near[:, C : 2 * C]], axis=0)
+                    put(e, plane, jnp.where(place == gap, 0.0, pltpu.roll(row, turn, 0)))
             for r in (0, Rm - 1):
                 depthwise(base, r, Pm)
             t, s = pointwise(layer, 0, 0, Rm, Pm, raw_d, 1)
         else:
+            act0(layer, 0, has_up)
+            act0(layer, Rm + 1, has_dn)
+            for e in range(1, Rm + 1):
+                act0(layer, e)
             t, s = convolve(layer, 0, 0, Rm, Pm, raw_d, 1)
         stats_begin(base, t, s, float(Rm * Wm))
         edge_d[0] = raw_d[1].astype(BF16)
@@ -362,6 +380,9 @@
         ]
         for m in edge:
             send(*m)
+        if layer == 0:
+            for m in mid_rows + top_rows:
+                send(*m)
         for m in edge:
             arrive(*m)
         raw_d[0] = red_d[layer, 0].astype(F32)
@@ -394,7 +415,8 @@
             (hb + 4, dn_f, rdn_f.at[layer], False),
         ]
         act1(0, has_up)
-        loop(1, part + 2, act1)
+        for e in range(1, part + 2):
+            act1(e)
         t, s = convolve(layer, 1, 0, part, Pf, raw_f)
         pool_cols_f(0)
         up_f[0] = cpf[0].astype(BF16)
@@ -421,6 +443,12 @@
             )
 
         loop(0, Rm - 1, pool_rows_f)
+        if layer == 0:
+            for m in mid_rows:
+                arrive(*m)
+            for p in range(Pm):
+                nm[0, p] = nm_r[0, p].astype(F32) * c0[0]
+                nm[Rm + 1, p] = nm_r[1, p].astype(F32) * c0[0]
         ratio_m = c2[0] / c0[0]
         ratio_d = c2[1] / c1[1]
 
@@ -445,7 +473,8 @@
 
         act2(0, has_up)
         act2(Rm + 1, has_dn)
-        loop(1, Rm + 1, act2)
+        for e in range(1, Rm + 1):
+            act2(e)
         t, s = convolve(layer, 2, 0, Rm, Pm, raw_m)
         stats_begin(base + 2, t, s, float(Rm * Wm))
 
@@ -516,6 +545,9 @@
             pool_m[Rt], jnp.where(has_dn, rup_m[layer, 0].astype(F32), -jnp.inf)
         )
         pool_m[Rt + 1] = rup_m[layer, 1].astype(F32)
+        if layer == 0:
+            for m in top_rows:
+                arrive(*m)
         sm = stats_end(base + 2, layer, 2)
 
         sw = scaled(sm, c3[1])
@@ -596,7 +628,7 @@
     V = pltpu.VMEM
     dw = jnp.transpose(dw, (0, 2, 3, 1, 4))
     w2 = jnp.swapaxes(w2, 1, 2)
-    messages = 4 + 15 * L
+    messages = 6 + 15 * L
     scratch = [
         V((Rf, Wf, C), BF16), V((Rm, Wm, C), BF16), V(w2.shape, F32), V(w3.shape, F32),
         V(pw.shape, BF16), V(dw.shape, BF16), V(gain.shape, F32), V(bias.shape, F32),
@@ -616,8 +648,8 @@
         V((L, 2, J, C), BF16), V((L, J, C), BF16),
         V((L, J, C), BF16), V((L, J, C), BF16), V((2, J, C), BF16),
         V((2, Wf, Wf), BF16), V((2, Wm, Wm), BF16),
-        V((L * NODES, nb * nr, 2, C), BF16),
-        pltpu.SemaphoreType.DMA((2, nb * nr)), pltpu.SemaphoreType.DMA((L * NODES, nb * nr)),
+        V((L * NODES, nb * nr, -(-2 * C // 1024) * 8, 128), BF16),
+        pltpu.SemaphoreType.DMA((2,)), pltpu.SemaphoreType.DMA((L * NODES,)),
         pltpu.SemaphoreType.DMA((messages,)), pltpu.SemaphoreType.DMA((messages,)),
         pltpu.SemaphoreType.DMA((9,)), pltpu.SemaphoreType.REGULAR((2,)),
     ]

time: 62.4 us -> 58.6 us (0.939)
  Pallas kernels: 61.6 us -> 57.8 us
    pallas_call x1, Pallas kernels: 60.5 us -> 56.6 us  [body(): pl.pallas_call(functools.partial(kernel, nb, nr), out_shape=[pltpu.VMEM(a...]
where the time goes in v1:
time: 58.6 us; the launch traced here: 58.4 us
  Pallas kernels  57.8 us (99%)
  between operations  0.64 us (1%)
    pallas_call x1, Pallas kernels, body(): pl.pallas_call(functools.partial(kernel, nb, nr), out_shape=[pltpu.VMEM(a...  56.6 us
    pallas_call x1, Pallas kernels, body(): pl.pallas_call(flush, out_shape=[jax.ShapeDtypeStruct(a.shape, BF16) for...  1.18 us

profile of v1, /device:TPU:0, one launch (start us, length us, event | category | flops | bytes accessed | tf_op | source)
XLA Modules:
  0.0 58.4 jit_solution(2071638049508893204)
XLA Ops:
  0.6 56.6 %bifpn.1 = (bf16[1,8,192,384]{3,2,1,0:T(8,128)(2,1)S(1)}, bf16[1,4,96,384]{3,2,1,0:T(8,128)(2,1)S(1)}, bf16[1,2,48,384]{3,2,1,0:T(8,128)(2,1)S(1)}) custom-call(bf16[1,8,192,384]{3,2,1,0:T(8,128)(2,1)} %fine.1, bf16[1,4,96,384]{3,2,1,0:T(8,128)(2,1)} %mid.1, bf16[1,2,48,384]{3,2,1,0:T(8,128)(2,1)} %top.1, f32[2,2,3]{2,1,0:T(2,128)} %bitcast.3, ...), custom_call_target="tpu_custom_call" | custom-call | tf_op jit(solution)/shard_map/bifpn/pallas_call | solution.py:658
  57.2 1.2 %flush.1 = (bf16[1,8,192,384]{3,2,1,0:T(8,128)(2,1)}, bf16[1,4,96,384]{3,2,1,0:T(8,128)(2,1)}, bf16[1,2,48,384]{3,2,1,0:T(8,128)(2,1)}) custom-call(bf16[1,8,192,384]{3,2,1,0:T(8,128)(2,1)S(1)} %get-tuple-element.6.a, bf16[1,4,96,384]{3,2,1,0:T(8,128)(2,1)S(1)} %get-tuple-element.7.b, bf16[1,2,48,384]{3,2,1,0:T(8,128)(2,1)S(1)} %get-tuple-element.8.c), custom_call_target="tpu_custom_call" | custom-call | tf_op jit(solution)/shard_map/flush/pallas_call | solution.py:669

commit v2 on v1

--- a/solution.py
+++ b/solution.py
@@ -368,8 +368,6 @@
         else:
             act0(layer, 0, has_up)
             act0(layer, Rm + 1, has_dn)
-            for e in range(1, Rm + 1):
-                act0(layer, e)
             t, s = convolve(layer, 0, 0, Rm, Pm, raw_d, 1)
         stats_begin(base, t, s, float(Rm * Wm))
         edge_d[0] = raw_d[1].astype(BF16)
@@ -383,10 +381,7 @@
         if layer == 0:
             for m in mid_rows + top_rows:
                 send(*m)
-        for m in edge:
-            arrive(*m)
-        raw_d[0] = red_d[layer, 0].astype(F32)
-        raw_d[Rm + 1] = red_d[layer, 1].astype(F32)
+        late = edge
         for m in fine_rows[2 * layer] + fine_rows[2 * layer + 1]:
             arrive(*m)
         for p in range(Pf):
@@ -398,7 +393,8 @@
             for p in range(Pm):
                 raw_d[e, p] = normal(raw_d[e, p], sd)
 
-        loop(0, Rm + 2, norm_d)
+        for e in range(1, Rm + 1):
+            norm_d(e)
 
         def act1(e, valid=None):
             for p in range(Pf):
@@ -408,15 +404,20 @@
             for q in range(Pm):
                 cpf[r, q] = column_pool(raw_f, r, q, Pf)
 
-        part = Rf // 2
+        part = Rf // 4
         edge = [
             (hb + 2, up_f.at[0], rup_f.at[layer, 0], True),
             (hb + 3, up_f.at[1], rup_f.at[layer, 1], True),
             (hb + 4, dn_f, rdn_f.at[layer], False),
         ]
-        act1(0, has_up)
         for e in range(1, part + 2):
             act1(e)
+        for m in late:
+            arrive(*m)
+        for p in range(Pm):
+            raw_d[0, p] = normal(red_d[layer, 0, p].astype(F32), sd)
+            raw_d[Rm + 1, p] = normal(red_d[layer, 1, p].astype(F32), sd)
+        act1(0, has_up)
         t, s = convolve(layer, 1, 0, part, Pf, raw_f)
         pool_cols_f(0)
         up_f[0] = cpf[0].astype(BF16)
@@ -457,13 +458,10 @@
                 raw_d[e, p] = nm[e, p] * ratio_m + raw_d[e, p] * ratio_d
 
         loop(0, Rm + 2, join_d)
-        for m in edge:
-            arrive(*m)
-        pool_f[0] = jnp.maximum(rdn_f[layer].astype(F32), cpf[0])
+        arrive(*edge[0])
         pool_f[Rm] = jnp.maximum(
             pool_f[Rm], jnp.where(has_dn, rup_f[layer, 0].astype(F32), -jnp.inf)
         )
-        pool_f[Rm + 1] = rup_f[layer, 1].astype(F32)
         sf = stats_end(base + 1, layer, 1)
         sw = scaled(sf, c2[2])
 
@@ -471,10 +469,14 @@
             for p in range(Pm):
                 activate(e, p, Pm, raw_d[e, p] + normal(pool_f[e, p], sw), valid)
 
+        for e in range(1, Rm + 1):
+            act2(e)
+        for m in edge[1:]:
+            arrive(*m)
+        pool_f[0] = jnp.maximum(rdn_f[layer].astype(F32), cpf[0])
+        pool_f[Rm + 1] = rup_f[layer, 1].astype(F32)
         act2(0, has_up)
         act2(Rm + 1, has_dn)
-        for e in range(1, Rm + 1):
-            act2(e)
         t, s = convolve(layer, 2, 0, Rm, Pm, raw_m)
         stats_begin(base + 2, t, s, float(Rm * Wm))
 
@@ -538,6 +540,18 @@
         if not last:
             for m in fine_rows[2 * layer + 2]:
                 send(*m)
+        if layer == 0:
+            for m in top_rows:
+                arrive(*m)
+        sm = stats_end(base + 2, layer, 2)
+        sw = scaled(sm, c3[1])
+
+        def act3(e, valid=None):
+            half = nt[layer, e].astype(F32) * c3[0] + normal(pool_m[e], sw)
+            activate(e, 0, 1, half, valid)
+
+        for e in range(1, Rt):
+            act3(e)
         for m in edge:
             arrive(*m)
         pool_m[0] = jnp.maximum(rdn_m[layer].astype(F32), cpm[0])
@@ -545,17 +559,9 @@
             pool_m[Rt], jnp.where(has_dn, rup_m[layer, 0].astype(F32), -jnp.inf)
         )
         pool_m[Rt + 1] = rup_m[layer, 1].astype(F32)
-        if layer == 0:
-            for m in top_rows:
-                arrive(*m)
-        sm = stats_end(base + 2, layer, 2)
-
-        sw = scaled(sm, c3[1])
-
-        for e in range(Rt + 2):
-            half = nt[layer, e].astype(F32) * c3[0] + normal(pool_m[e], sw)
-            valid = has_up if e == 0 else has_dn if e == Rt + 1 else None
-            activate(e, 0, 1, half, valid)
+        act3(Rt)
+        act3(0, has_up)
+        act3(Rt + 1, has_dn)
         t, s = convolve(layer, 3, 0, Rt, 1, raw_t)
         stats_begin(base + 3, t, s, float(Rt * J))
         if last:
@@ -589,15 +595,17 @@
                     nm[r + 1, p] = normal(raw_m[r, p, pl.ds(0, J), :], sn)
 
             loop(0, Rm, finish_m)
+            st = stats_end(base + 3, layer, 3)
+            for r in range(Rt):
+                nt[layer + 1, r + 1] = normal(raw_t[r, 0], st).astype(BF16)
+            for e in range(1, Rm + 1):
+                act0(layer + 1, e)
             for m in edge + rows:
                 arrive(*m)
             for p in range(Pm):
                 nm[0, p] = normal(red_m[layer, 0, p].astype(F32), sn)
                 nm[Rm + 1, p] = normal(red_m[layer, 1, p].astype(F32), sn)
-            st = stats_end(base + 3, layer, 3)
             nt[layer + 1, 0] = normal(rdn_t[layer].astype(F32), st).astype(BF16)
-            for r in range(Rt):
-                nt[layer + 1, r + 1] = normal(raw_t[r, 0], st).astype(BF16)
             nt[layer + 1, Rt + 1] = normal(rup_t[layer].astype(F32), st).astype(BF16)
 
 

time: 58.6 us -> 57.9 us (0.988)
  Pallas kernels: 57.8 us -> 57.1 us
    pallas_call x1, Pallas kernels: 56.6 us -> 55.9 us  [body(): pl.pallas_call(functools.partial(kernel, nb, nr), out_shape=[pltpu.VMEM(a...]
where the time goes in v2:
time: 57.9 us; the launch traced here: 57.7 us
  Pallas kernels  57.1 us (99%)
  between operations  0.64 us (1%)
    pallas_call x1, Pallas kernels, body(): pl.pallas_call(functools.partial(kernel, nb, nr), out_shape=[pltpu.VMEM(a...  55.9 us
    pallas_call x1, Pallas kernels, body(): pl.pallas_call(flush, out_shape=[jax.ShapeDtypeStruct(a.shape, BF16) for...  1.18 us

profile of v2, /device:TPU:0, one launch (start us, length us, event | category | flops | bytes accessed | tf_op | source)
XLA Modules:
  0.0 57.7 jit_solution(4919024590524807436)
XLA Ops:
  0.6 55.9 %bifpn.1 = (bf16[1,8,192,384]{3,2,1,0:T(8,128)(2,1)S(1)}, bf16[1,4,96,384]{3,2,1,0:T(8,128)(2,1)S(1)}, bf16[1,2,48,384]{3,2,1,0:T(8,128)(2,1)S(1)}) custom-call(bf16[1,8,192,384]{3,2,1,0:T(8,128)(2,1)} %fine.1, bf16[1,4,96,384]{3,2,1,0:T(8,128)(2,1)} %mid.1, bf16[1,2,48,384]{3,2,1,0:T(8,128)(2,1)} %top.1, f32[2,2,3]{2,1,0:T(2,128)} %bitcast.3, ...), custom_call_target="tpu_custom_call" | custom-call | tf_op jit(solution)/shard_map/bifpn/pallas_call | solution.py:666
  56.5 1.2 %flush.1 = (bf16[1,8,192,384]{3,2,1,0:T(8,128)(2,1)}, bf16[1,4,96,384]{3,2,1,0:T(8,128)(2,1)}, bf16[1,2,48,384]{3,2,1,0:T(8,128)(2,1)}) custom-call(bf16[1,8,192,384]{3,2,1,0:T(8,128)(2,1)S(1)} %get-tuple-element.6.a, bf16[1,4,96,384]{3,2,1,0:T(8,128)(2,1)S(1)} %get-tuple-element.7.b, bf16[1,2,48,384]{3,2,1,0:T(8,128)(2,1)S(1)} %get-tuple-element.8.c), custom_call_target="tpu_custom_call" | custom-call | tf_op jit(solution)/shard_map/flush/pallas_call | solution.py:677
